TPU v7x, 32 devices: a whole 2x2x4 slice. The times are simulated.
32 devices in a mesh: dp: 32 (over z, y, x, core).
Axes of the slice: x: 2, y: 2, z: 4, core: 2. Of those that a mesh axis runs over, the one named last changes fastest.
Arguments:
- grad_qkv: bfloat16 [64, 768, 2304], P('dp')
- grad_o: bfloat16 [64, 768, 768], P('dp')
- grad_up: bfloat16 [64, 768, 3072], P('dp')
- grad_down: bfloat16 [64, 3072, 768], P('dp')
- w_qkv: float32 [2, 768, 2304], replicated
- w_o: float32 [2, 768, 768], replicated
- w_up: float32 [2, 768, 3072], replicated
- w_down: float32 [2, 3072, 768], replicated
- stat_left: float32 [7, 32, 256, 256], P(None, 'dp')
- stat_right: float32 [7, 32, 256, 256], P(None, 'dp')
- graft_var: float32 [7, 32, 256, 256], P(None, 'dp')
Outputs:
- output 1: float32 [2, 768, 2304], replicated
- output 2: float32 [2, 768, 768], replicated
- output 3: float32 [2, 768, 3072], replicated
- output 4: float32 [2, 3072, 768], replicated
- output 5: float32 [7, 32, 256, 256], P(None, 'dp')
- output 6: float32 [7, 32, 256, 256], P(None, 'dp')
- output 7: float32 [7, 32, 256, 256], P(None, 'dp')
All inputs are finite; a program needn't handle non-finite values.
Results may differ from a plain program's by a relative error of at most 0.001.
Values sent between devices are 32-bit elements.
A program may use at most 1 GiB of HBM per device.

v0:
```python
import jax
import jax.numpy as jnp
from jax import lax
from jax.sharding import PartitionSpec as P

STAT_BETA = 0.999
EPS_ROOT = 1e-6
EPS_GRAFT = 1e-8
LR_RATE = 1e-3
WEIGHT_DECAY = 0.01
NEWTON_ITERS = 15
STEP_COUNT = 100
BIAS_FIX = 1.0 - STAT_BETA ** STEP_COUNT


def product(form, left_op, right_op):
    return jnp.einsum(form, left_op, right_op, precision=lax.Precision.HIGHEST, preferred_element_type=jnp.float32)


def inverse_root(stat_mat):
    identity = jnp.eye(stat_mat.shape[-1], dtype=jnp.float32)
    shifted = stat_mat + EPS_ROOT * identity
    frob_norm = jnp.sqrt(jnp.sum(shifted * shifted, axis=(-2, -1), keepdims=True))

    def newton_step(index, newton_state):
        root_x, mat_m = newton_state
        factor = (5.0 * identity - mat_m) / 4.0
        factor_sq = product('...ij,...jk->...ik', factor, factor)
        return (product('...ij,...jk->...ik', root_x, factor), product('...ij,...jk->...ik', product('...ij,...jk->...ik', factor_sq, factor_sq), mat_m))

    root_x, mat_m = lax.fori_loop(0, NEWTON_ITERS, newton_step, (identity * frob_norm ** -0.25, shifted / frob_norm))
    return root_x


def update_stats(grad_block, left_stat, right_stat, var_stat):
    left_new = STAT_BETA * left_stat + (1.0 - STAT_BETA) * product('...ij,...kj->...ik', grad_block, grad_block)
    right_new = STAT_BETA * right_stat + (1.0 - STAT_BETA) * product('...ji,...jk->...ik', grad_block, grad_block)
    var_new = STAT_BETA * var_stat + (1.0 - STAT_BETA) * grad_block * grad_block
    return left_new, right_new, var_new


def grafted_direction(grad_block, left_new, right_new, var_new):
    precond = product('...ij,...jk->...ik', product('...ij,...jk->...ik', inverse_root(left_new), grad_block), inverse_root(right_new))
    adam_dir = grad_block / (jnp.sqrt(var_new / BIAS_FIX) + EPS_GRAFT)
    adam_sq = jnp.sum(adam_dir * adam_dir, axis=(-2, -1), keepdims=True)
    precond_sq = jnp.sum(precond * precond, axis=(-2, -1), keepdims=True)
    return precond * (jnp.sqrt(adam_sq) / jnp.sqrt(precond_sq))


def to_blocks(matrices, block_dim):
    pieces = []
    for matrix in matrices:
        layers, n_rows, n_cols = matrix.shape
        tiled = matrix.reshape(layers, n_rows // block_dim, block_dim, n_cols // block_dim, block_dim)
        pieces.append(tiled.transpose(0, 1, 3, 2, 4).reshape(layers, -1, block_dim, block_dim))
    return jnp.concatenate(pieces, axis=1).reshape(-1, block_dim, block_dim)


def from_blocks(blocks, mat_shapes, block_dim):
    layers = mat_shapes[0][0]
    per_layer = blocks.reshape(layers, -1, block_dim, block_dim)
    matrices = []
    offset = 0
    for mat_shape in mat_shapes:
        n_rows, n_cols = mat_shape[1], mat_shape[2]
        tile_count = (n_rows // block_dim) * (n_cols // block_dim)
        tiled = per_layer[:, offset:offset + tile_count].reshape(layers, n_rows // block_dim, n_cols // block_dim, block_dim, block_dim)
        matrices.append(tiled.transpose(0, 1, 3, 2, 4).reshape(layers, n_rows, n_cols))
        offset = offset + tile_count
    return matrices


def solution(mesh):
    ranks = mesh.shape['dp']

    def local_step(grad_qkv, grad_o, grad_up, grad_down, w_qkv, w_o, w_up, w_down, left_stat, right_stat, var_stat):
        block_dim = left_stat.shape[-1]
        slots = left_stat.shape[0]
        weights = (w_qkv, w_o, w_up, w_down)
        grad_blocks = to_blocks((grad_qkv, grad_o, grad_up, grad_down), block_dim).astype(jnp.float32)
        total = grad_blocks.shape[0]
        padded = jnp.pad(grad_blocks, ((0, slots * ranks - total), (0, 0), (0, 0)))
        mean_blocks = lax.psum_scatter(padded.reshape(slots, ranks, block_dim, block_dim), 'dp', scatter_dimension=1, tiled=True) / ranks
        left_new, right_new, var_new = update_stats(mean_blocks, left_stat, right_stat, var_stat)
        direction = grafted_direction(mean_blocks, left_new, right_new, var_new)
        owned = jnp.arange(slots) * ranks + lax.axis_index('dp')
        valid = (owned < total)[:, None, None, None]
        direction = jnp.where(valid, direction, 0.0)
        gathered = lax.all_gather(direction, 'dp', axis=1, tiled=True).reshape(slots * ranks, block_dim, block_dim)[:total]
        step_dirs = from_blocks(gathered, [weight.shape for weight in weights], block_dim)
        new_weights = tuple(weight - LR_RATE * (step_dir + WEIGHT_DECAY * weight) for weight, step_dir in zip(weights, step_dirs))
        return new_weights + (jnp.where(valid, left_new, left_stat), jnp.where(valid, right_new, right_stat), jnp.where(valid, var_new, var_stat))

    grad_spec = P('dp')
    stat_spec = P(None, 'dp')
    return jax.shard_map(local_step, mesh=mesh, in_specs=(grad_spec,) * 4 + (P(),) * 4 + (stat_spec,) * 3, out_specs=(P(),) * 4 + (stat_spec,) * 3, check_vma=False)
```

profile of v0, /device:TPU:0, one launch (start us, length us, event | category | flops | bytes accessed | tf_op | source)
XLA Modules:
  0.0 1882.4 jit_solution(14819388306350527556)
XLA Ops:
  7.2 12.6 copy.44
  19.8 17.2 reshape.242
  37.0 16.3 copy.45
  53.3 10.3 copy.40
  63.6 16.3 reshape.236
  79.9 14.5 copy.41
  94.4 17.2 reshape.240
  111.6 12.1 copy.43
  130.1 19.4 %pad_maximum_fusion = bf16[2,108,256,256]{3,2,1,0:T(8,128)(2,1)} fusion(bf16[2,36,256,256]{3,2,1,0:T(8,128)(2,1)} %bitcast.192, bf16[2,36,256,256]{3,2,1,0:T(8,128)(2,1)} %bitcast.193, bf16[2,9,256,256]{3,2,1,0:T(8,128)(2,1)} %bitcast.198, bf16[2,27,256,256]{3,2,1,0:T(8,128)(2,1)} %bitcast.195), kind=kLoop, calls=%fused_computation.38 | loop fusion | flops 42467328 | bytes 56623104 | tf_op jit(solution)/shard_map/concatenate | solution.py:56
  149.5 19.7 %pad.5 = bf16[224,256,256]{2,1,0:T(8,128)(2,1)} pad(bf16[216,256,256]{2,1,0:T(8,128)(2,1)} %bitcast.185, bf16[]{:T(256)} %constant.17.clone.1), padding=0_8x0_0x0_0 | pad | bytes 57671680 | tf_op jit(solution)/shard_map/jit(_pad)/pad | solution.py:82
  169.2 28.2 %copy.46 = f32[7,32,256,256]{3,2,0,1:T(8,128)} copy(bf16[7,32,256,256]{3,2,1,0:T(8,128)(2,1)} %bitcast.184) | data formatting | bytes 88080384 | tf_op jit(solution)/shard_map/reshape | solution.py:83
  197.9 617.0 %reduce-scatter.2.cloned.1.call-done = f32[7,1,256,256]{3,2,0,1:T(8,128)} async-done(((f32[7,32,256,256]{3,2,0,1:T(8,128)}), f32[7,1,256,256]{3,2,0,1:T(8,128)}) %reduce-scatter.2.cloned.1.call-update) | async-done | bytes 1835024 | tf_op jit(solution)/shard_map/reduce_scatter | solution.py:83
  830.8 180.4 %while.27 = (s32[]{:T(128)}, f32[7,1,256,256]{2,3,0,1:T(8,128)S(1)}, f32[7,1,256,256]{3,2,0,1:T(8,128)}, s32[]{:T(128)}) while((s32[]{:T(128)}, f32[7,1,256,256]{2,3,0,1:T(8,128)S(1)}, f32[7,1,256,256]{3,2,0,1:T(8,128)}, s32[]{:T(128)}) %tuple.64), condition=%wide.region_6.7_spmd.clone, body=%wide.region_5.6_spmd.clone.sunk | while | flops 5639110656 | bytes 26476596 | solution.py:31
  1011.1 206.4 %while.26 = (s32[]{:T(128)}, f32[7,1,256,256]{2,3,0,1:T(8,128)}, f32[7,1,256,256]{3,2,0,1:T(8,128)}, s32[]{:T(128)}) while((s32[]{:T(128)}, f32[7,1,256,256]{2,3,0,1:T(8,128)}, f32[7,1,256,256]{3,2,0,1:T(8,128)}, s32[]{:T(128)}) %tuple.61), condition=%wide.region_3.4_spmd.clone, body=%wide.region_2.3_spmd.clone.sunk | while | flops 5639110656 | bytes 33816656 | solution.py:31
  1226.3 18.6 copy.58
  1244.9 15.1 copy.53
  1260.0 290.7 %all-gather.3.cloned.1.call-done = f32[7,8192,256]{2,1,0:T(8,128)} async-done(((f32[7,256,256]{2,1,0:T(8,128)}), f32[7,8192,256]{2,1,0:T(8,128)}) %all-gather.3.cloned.1.call-update) | async-done | bytes 58720272 | tf_op jit(solution)/shard_map/all_gather | solution.py:89
  1550.8 38.5 %slice.20 = f32[216,256,256]{2,1,0:T(8,128)} slice(f32[224,256,256]{2,1,0:T(8,128)} %bitcast.189), slice={[0:216], [0:256], [0:256]} | slice | bytes 113246208 | tf_op jit(solution)/shard_map/slice | solution.py:89
  1589.3 24.3 %fusion.76 = (f32[2,36,256,256]{3,2,1,0:T(8,128)}, f32[2,36,256,256]{3,2,1,0:T(8,128)}) fusion(f32[2,108,256,256]{3,2,1,0:T(8,128)} %bitcast.181), kind=kLoop, calls=%fused_computation.89 | loop fusion | bytes 75497472 | tf_op jit(solution)/shard_map/slice | solution.py:67
  1613.5 11.6 slice.21
  1630.0 22.4 %copy.56 = f32[2,12,256,3,256]{2,1,4,3,0:T(8,128)} copy(f32[2,12,256,3,256]{4,2,3,1,0:T(8,128)} %bitcast.187) | data formatting | bytes 37748736 | tf_op jit(solution)/shard_map/transpose | solution.py:68
  1652.4 23.1 %reshape.258 = f32[2,3072,768]{1,2,0:T(8,128)} reshape(f32[2,12,256,3,256]{2,1,4,3,0:T(8,128)} %copy.56) | data formatting | bytes 37748736 | tf_op jit(solution)/shard_map/reshape | solution.py:68
  1675.5 20.8 %multiply_subtract_fusion = f32[2,3072,768]{1,2,0:T(8,128)} fusion(f32[2,3072,768]{1,2,0:T(8,128)} %copy.58, f32[2,3072,768]{1,2,0:T(8,128)} %reshape.258), kind=kLoop, calls=%fused_computation.39 | loop fusion | flops 18874368 | bytes 56623104 | tf_op jit(solution)/shard_map/sub | solution.py:91
  1696.3 18.6 copy.63
  1714.9 22.0 %copy.55 = f32[2,3,256,12,256]{4,3,2,1,0:T(8,128)} copy(f32[2,3,256,12,256]{4,2,3,1,0:T(8,128)} %bitcast.186) | data formatting | bytes 37748736 | tf_op jit(solution)/shard_map/transpose | solution.py:68
  1736.9 23.2 %reshape.256 = f32[2,768,3072]{2,1,0:T(8,128)} reshape(f32[2,3,256,12,256]{4,3,2,1,0:T(8,128)} %copy.55) | data formatting | bytes 37748736 | tf_op jit(solution)/shard_map/reshape | solution.py:68
  1760.1 19.6 %copy.51 = f32[2,3,256,9,256]{2,1,4,3,0:T(4,128)} copy(f32[2,3,256,9,256]{4,2,3,1,0:T(8,128)} %bitcast.188) | data formatting | bytes 28311552 | tf_op jit(solution)/shard_map/transpose | solution.py:68
  1779.7 22.9 %reshape.252 = f32[2,768,2304]{1,2,0:T(8,128)} reshape(f32[2,3,256,9,256]{2,1,4,3,0:T(4,128)} %copy.51) | data formatting | bytes 28311552 | tf_op jit(solution)/shard_map/reshape | solution.py:68
  1802.7 15.0 multiply_subtract_fusion.2
  1817.7 15.3 copy.62
  1841.2 8.4 reshape.254
  1849.7 22.7 %multiply_subtract_fusion.1 = f32[2,768,3072]{2,1,0:T(8,128)} fusion(f32[2,768,3072]{2,1,0:T(8,128)} %param.21, f32[2,768,3072]{2,1,0:T(8,128)} %reshape.256), kind=kLoop, calls=%fused_computation.40 | loop fusion | flops 18874368 | bytes 56623104 | tf_op jit(solution)/shard_map/sub | solution.py:91
  (279 shorter events, 432.6 us)
Async XLA Ops:
  7.2 807.7 %reduce-scatter.2.cloned.1.call-start = ((), (), s32[]{:S(2)}) async-start(), calls=%async_computation.1 | async-start | bytes 60555264 | tf_op jit(solution)/shard_map/reduce_scatter | solution.py:83
  197.4 617.4 %copy-start.3 = (f32[7,1,256,256]{3,2,1,0:T(8,128)S(1)}, f32[7,1,256,256]{3,2,1,0:T(8,128)}, u32[]{:S(2)}) copy-start(f32[7,1,256,256]{3,2,1,0:T(8,128)} %param.23) | copy-start | bytes 5505028
  197.5 1353.3 %all-gather.3.cloned.1.call-start = ((), (), s32[]{:S(2)}) async-start(), calls=%async_computation.2 | async-start | bytes 60555264 | tf_op jit(solution)/shard_map/all_gather | solution.py:89
  814.9 4.3 copy-start.1
  814.9 4.3 copy-start.5
  822.7 1.8 copy-start.4
  822.7 2.7 copy-start.6
  1011.5 2.1 copy-start
  1025.3 2.1 copy-start
  1039.0 2.1 copy-start
  1052.7 2.1 copy-start
  1066.4 2.1 copy-start
  1080.2 2.1 copy-start
  1093.9 2.1 copy-start
  1107.6 2.1 copy-start
  1121.3 2.1 copy-start
  1135.1 2.1 copy-start
  1148.8 2.1 copy-start
  1162.5 2.1 copy-start
  1176.2 2.1 copy-start
  1189.9 2.1 copy-start
  1203.7 2.1 copy-start
  1841.2 31.1 %slice-start = ((s8[4718592]{0:T(1024)(128)(4,1)}), s8[524288]{0:T(1024)(128)(4,1)S(1)}, s32[]{:S(2)}) async-start(s8[4718592]{0:T(1024)(128)(4,1)} %bitcast.199), calls=%async_computation.3 | async-start | bytes 1048576
  1849.7 22.7 %copy-start.2 = (f32[2,768,768]{2,1,0:T(8,128)S(1)}, f32[2,768,768]{2,1,0:T(8,128)}, u32[]{:S(2)}) copy-start(f32[2,768,768]{2,1,0:T(8,128)} %reshape.254) | copy-start | bytes 14155780
  1849.7 22.7 %slice-start.1 = ((s8[4718592]{0:T(1024)(128)(4,1)}), s8[4194304]{0:T(1024)(128)(4,1)S(1)}, s32[]{:S(2)}) async-start(s8[4718592]{0:T(1024)(128)(4,1)} %bitcast.199), calls=%async_computation.4 | async-start | bytes 8388608
Sparse Core Ops, SparseCore 0:
  197.6 617.2 reduce-scatter.1
  1226.4 324.2 all-gather.2
where the time goes:
time: 1900 us; the launch traced here: 1880 us
  waiting for transfers between devices  908 us (48%)
  local copies, waits for them, and re-layouts  526 us (28%)
  matrix products  342 us (18%)
  other arithmetic  89.8 us (5%)
    reduce_scatter x1, waiting for transfers between devices, local_step(): lax.psum_scatter(padded.reshape(slots, ranks, block_dim, block_dim), 'dp'...  617 us
    dot_general x124, matrix products, product(): jnp.einsum(form, left_op, right_op, precision=lax.Precision.HIGHEST, pref...  342 us
    all_gather x1, waiting for transfers between devices, local_step(): lax.all_gather(direction, 'dp', axis=1, tiled=True)  291 us
    unnamed x22, local copies, waits for them, and re-layouts  91.6 us
    reshape x4, local copies, waits for them, and re-layouts, from_blocks(): tiled.transpose(0, 1, 3, 2, 4).reshape(layers, n_rows, n_cols)  77.7 us
    transpose x4, local copies, waits for them, and re-layouts, from_blocks(): tiled.transpose(0, 1, 3, 2, 4).reshape(layers, n_rows, n_cols)  72.3 us
    sub x4, other arithmetic, local_step(): weight - LR_RATE * (step_dir + WEIGHT_DECAY * weight)  61.4 us
    while x90, local copies, waits for them, and re-layouts  57.2 us
  transfers between devices with their start and end apart: 2, of which 2 were waited for; matrix products, arithmetic and copies ran while one was open for 2% of the time, Pallas kernels for 0%

commit v1 on v0

v1 whole, which is shorter than its diff:
```python
import functools

import jax
import jax.numpy as jnp
from jax import lax
from jax.experimental import pallas as pl
from jax.experimental.pallas import tpu as pltpu
from jax.sharding import PartitionSpec as P

STAT_BETA = 0.999
EPS_ROOT = 1e-6
EPS_GRAFT = 1e-8
LR_RATE = 1e-3
WEIGHT_DECAY = 0.01
NEWTON_ITERS = 15
STEP_COUNT = 100
BIAS_FIX = 1.0 - STAT_BETA ** STEP_COUNT

RANKS = 32
HALVES = 2
MESH = pl.DeviceIdType.MESH
F32 = jnp.float32


def flipped(bit, flip):
    return bit + flip - 2 * bit * flip


def place():
    me = lax.axis_index('dp')
    core = me % 2
    x, y, za, zb = (me // 2) % 2, (me // 4) % 2, (me // 8) % 2, me // 16
    stride1, bit1 = 2 + 2 * core, x + core * (y - x)
    stride3, bit3 = 4 - 2 * core, y + core * (x - y)
    partners = (
        me + 1 - 2 * core,
        me + stride1 * (1 - 2 * bit1),
        me + 8 * (1 - 2 * za),
        me + stride3 * (1 - 2 * bit3),
        me + 16 * (1 - 2 * zb),
    )
    return me, (core, x, y, za, zb), partners


def owner_at(coords, pos, core):
    _, x, y, za, zb = coords
    b1, b2, b3, b4 = (pos // 8) % 2, (pos // 4) % 2, (pos // 2) % 2, pos % 2
    fx, fy = b1 + core * (b3 - b1), b3 + core * (b1 - b3)
    return flipped(zb, b4) * 16 + flipped(za, b2) * 8 + flipped(y, fy) * 4 + flipped(x, fx) * 2 + core


class Tiling:
    def __init__(self, shapes, block):
        self.block = block
        self.layers = shapes[0][0]
        self.spans = []
        start = 0
        for _, rows, cols in shapes:
            count = (rows // block) * (cols // block)
            self.spans.append((start, start + count, cols // block))
            start += count
        self.per_layer = start
        self.total = start * self.layers

    def visit(self, number, half, fn):
        layer, local = number // self.per_layer, number % self.per_layer
        rows = self.block // HALVES
        for index, (low, high, width) in enumerate(self.spans):
            @pl.when((local >= low) & (local < high))
            def _():
                row, col = (local - low) // width, (local - low) % width
                fn(index, layer, pl.ds(pl.multiple_of(row * self.block + half * rows, rows), rows),
                   pl.ds(pl.multiple_of(col * self.block, self.block), self.block))


def enter(partners):
    barrier = pltpu.get_barrier_semaphore()
    for partner in partners:
        pl.semaphore_signal(barrier, inc=1, device_id=(partner,), device_id_type=MESH)
    pl.semaphore_wait(barrier, len(partners))


def split(value):
    high = value.astype(jnp.bfloat16)
    rest = value - high.astype(F32)
    mid = rest.astype(jnp.bfloat16)
    return high, mid, (rest - mid.astype(F32)).astype(jnp.bfloat16)


def pieces(left, right):
    return jnp.dot(left, right, preferred_element_type=F32)


def product(left, right):
    a1, a2, a3 = left
    b1, b2, b3 = right
    return (pieces(a3, b1) + pieces(a2, b2) + pieces(a1, b3) + pieces(a2, b1) + pieces(a1, b2)) + pieces(a1, b1)


def total(value):
    return jnp.sum(jnp.sum(value, axis=0, keepdims=True), axis=1, keepdims=True)


TICKS = 15
HALF_STEP = 8
OFFSETS = {'load': 0, 'e0': 2, 'e1': 5, 'e2': 15, 'e3': 25, 'e4': 30, 'e5': 35}
LATENCY = 3
N_SEND, N_A, N_B, N_ACC, N_RECV = 2, 2, 3, 6, 4


def reduce_kernel(tiling, slots, g_qkv, g_o, g_up, g_down, l_in, r_in, v_in, l_out, r_out, v_out, u_out,
                  a_buf, b_buf, send0, acc, recv1, recv2, recv3, recv4, grad, stats, staged, u_buf, xs, ms, norms,
                  load_sem, send_sem, recv_sem, stat_sem, out_sem, u_sem):
    me, coords, partners = place()
    core = coords[0]
    block = tiling.block
    rows = block // HALVES
    units = slots * HALVES
    grads = (g_qkv, g_o, g_up, g_down)
    recvs = (None, recv1, recv2, recv3, recv4)

    def loads(unit, which):
        return pltpu.make_async_copy((a_buf, b_buf)[which].at[unit % (N_A, N_B)[which]],
                                     (a_buf, b_buf)[which].at[unit % (N_A, N_B)[which]],
                                     load_sem.at[which, unit % (N_A, N_B)[which]])

    def remote(stage, unit):
        slot = unit % N_ACC
        if stage == 0:
            src, dst = send0.at[unit % N_SEND], acc.at[slot]
        else:
            size = 16 >> stage
            src, dst = acc.at[slot, pl.ds(size, size)], recvs[stage].at[unit % N_RECV]
        return pltpu.make_async_remote_copy(src, dst, send_sem.at[stage, slot], recv_sem.at[stage, slot],
                                            device_id=(partners[stage],), device_id_type=MESH)

    def load(unit):
        slot, half = unit // HALVES, unit % HALVES

        def one(pos, _):
            for which, owner_core in ((0, 1 - core), (1, core)):
                number = slot * RANKS + owner_at(coords, pos, owner_core)
                number = number - RANKS * (number // tiling.total)
                buf, n = ((a_buf, N_A), (b_buf, N_B))[which]

                def start(index, layer, rws, cls):
                    pltpu.make_async_copy(grads[index].at[layer, rws, cls], buf.at[unit % n, pos],
                                          load_sem.at[which, unit % n]).start()
                tiling.visit(number, half, start)
            return 0
        lax.fori_loop(0, 16, one, 0)

    def e0(unit):
        loads(unit, 0).wait()

        def one(pos, _):
            send0[unit % N_SEND, pos] = a_buf[unit % N_A, pos].astype(F32)
            return 0
        lax.fori_loop(0, 16, one, 0)
        remote(0, unit).start()

    def e1(unit):
        loads(unit, 1).wait()
        remote(0, unit).wait()

        def one(back, _):
            pos = 15 - back
            acc[unit % N_ACC, pos] += b_buf[unit % N_B, pos].astype(F32)
            return 0
        lax.fori_loop(0, 16, one, 0)
        remote(1, unit).start()

    def step(stage, unit):
        remote(stage, unit).wait()
        size = 16 >> stage

        def one(back, _):
            pos = size - 1 - back
            acc[unit % N_ACC, pos] += recvs[stage][unit % N_RECV, pos]
            return 0
        lax.fori_loop(0, size, one, 0)
        remote(stage + 1, unit).start()

    def e5(unit):
        remote(4, unit).wait()
        half = unit % HALVES
        grad[(unit // HALVES) % 2, pl.ds(pl.multiple_of(half * rows, rows), rows), :] = (
            acc[unit % N_ACC, 0] + recv4[unit % N_RECV, 0]) * (1.0 / RANKS)

    events = {'load': load, 'e0': e0, 'e1': e1, 'e2': functools.partial(step, 1), 'e3': functools.partial(step, 2),
              'e4': functools.partial(step, 3), 'e5': e5}

    def stat_copies(slot):
        return [pltpu.make_async_copy(ref.at[slot], stats.at[i], stat_sem.at[i]) for i, ref in enumerate((l_in, r_in, v_in))]

    def out_copies(slot):
        return [pltpu.make_async_copy(staged.at[i], ref.at[slot], out_sem.at[i]) for i, ref in enumerate((l_out, r_out, v_out))]

    def u_copy(slot):
        return pltpu.make_async_copy(u_buf, u_out.at[slot], u_sem)

    row_id = lax.broadcasted_iota(jnp.int32, (block, block), 0)
    col_id = lax.broadcasted_iota(jnp.int32, (block, block), 1)

    def ident():
        return jnp.where(row_id == col_id, 1.0, 0.0).astype(F32)

    def factor(mat):
        return (5.0 * ident() - mat) * 0.25

    def power4(parts):
        square = split(product(parts, parts))
        return split(product(square, square))

    def before(slot):
        for copy in stat_copies(slot):
            copy.wait()
        valid = slot * RANKS + me < tiling.total
        g = grad[slot % 2]
        g_parts, gt_parts = split(g), split(g.T)
        var = stats[2]
        var_new = STAT_BETA * var + (1.0 - STAT_BETA) * g * g
        staged[2] = jnp.where(valid, var_new, var)
        adam = g / (jnp.sqrt(var_new / BIAS_FIX) + EPS_GRAFT)
        norms[...] = jnp.broadcast_to(jnp.sqrt(total(adam * adam)), norms.shape)
        for i, (left, right) in enumerate(((g_parts, gt_parts), (gt_parts, g_parts))):
            old = stats[i]
            new = STAT_BETA * old + (1.0 - STAT_BETA) * product(left, right)
            staged[i] = jnp.where(valid, new, old)
            shifted = new + EPS_ROOT * ident()
            frob = jnp.sqrt(total(shifted * shifted))
            mat = shifted / frob
            t = factor(mat)
            xs[i] = lax.rsqrt(jnp.sqrt(frob)) * t
            ms[i] = product(power4(split(t)), split(mat))

    def newton():
        ts = [split(factor(ms[i])) for i in range(2)]
        squares = [split(product(t, t)) for t in ts]
        for i in range(2):
            xs[i] = product(split(xs[i]), ts[i])
        fourths = [split(product(sq, sq)) for sq in squares]
        for i in range(2):
            ms[i] = product(fourths[i], split(ms[i]))

    def after(slot):
        roots = [split(product(split(xs[i]), split(factor(ms[i])))) for i in range(2)]
        g_parts = split(grad[slot % 2])
        precond = product(split(product(roots[0], g_parts)), roots[1])
        scale = norms[0:1, 0:1] / jnp.sqrt(total(precond * precond))
        u_buf[...] = precond * scale

    def compute(slot, tick):
        inside = (slot >= 0) & (slot < slots)

        @pl.when(inside & (tick == 0))
        def _():
            before(slot)

        @pl.when(inside & (tick > 0) & (tick < TICKS - 1))
        def _():
            newton()

        @pl.when(inside & (tick == TICKS - 1))
        def _():
            after(slot)

        @pl.when(inside & (tick == 1))
        def _():
            for copy in out_copies(slot):
                copy.start()

        @pl.when((slot >= -1) & (slot < slots - 1) & (tick == 2))
        def _():
            for copy in stat_copies(slot + 1):
                copy.start()

        @pl.when(inside & (tick == TICKS - 2))
        def _():
            for copy in out_copies(slot):
                copy.wait()

        @pl.when((slot >= 1) & (slot < slots) & (tick == 1))
        def _():
            u_copy(slot - 1).start()

        @pl.when((slot >= 1) & (slot < slots) & (tick == TICKS - 2))
        def _():
            u_copy(slot - 1).wait()

    enter(partners)

    def period(s, _):
        def one_tick(tick, _):
            for name in ('e5', 'e4', 'e3', 'e2', 'e1', 'e0', 'load'):
                for half in range(HALVES):
                    offset = OFFSETS[name] + HALF_STEP * half
                    slot = s - offset // TICKS

                    @pl.when((tick == offset % TICKS) & (slot >= 0) & (slot < slots))
                    def _(name=name, half=half, slot=slot):
                        events[name](slot * HALVES + half)
            compute(s - LATENCY, tick)
            return 0
        lax.fori_loop(0, TICKS, one_tick, 0)
        return 0
    lax.fori_loop(0, slots + LATENCY, period, 0)
    u_copy(slots - 1).start()
    u_copy(slots - 1).wait()


def reduce_and_direct(tiling, grads, stats, collective_id):
    slots, block = stats[0].shape[0], tiling.block
    rows = block // HALVES
    stat_shape = jax.ShapeDtypeStruct((slots, block, block), F32)
    hbm = pl.BlockSpec(memory_space=pl.ANY)
    dma = pltpu.SemaphoreType.DMA
    return pl.pallas_call(
        functools.partial(reduce_kernel, tiling, slots),
        out_shape=[stat_shape] * 4,
        in_specs=[hbm] * 7,
        out_specs=[hbm] * 4,
        scratch_shapes=[
            pltpu.VMEM((N_A, 16, rows, block), jnp.bfloat16),
            pltpu.VMEM((N_B, 16, rows, block), jnp.bfloat16),
            pltpu.VMEM((N_SEND, 16, rows, block), F32),
            pltpu.VMEM((N_ACC, 16, rows, block), F32),
            pltpu.VMEM((N_RECV, 8, rows, block), F32),
            pltpu.VMEM((N_RECV, 4, rows, block), F32),
            pltpu.VMEM((N_RECV, 2, rows, block), F32),
            pltpu.VMEM((N_RECV, 1, rows, block), F32),
            pltpu.VMEM((2, block, block), F32),
            pltpu.VMEM((3, block, block), F32),
            pltpu.VMEM((3, block, block), F32),
            pltpu.VMEM((block, block), F32),
            pltpu.VMEM((2, block, block), F32),
            pltpu.VMEM((2, block, block), F32),
            pltpu.VMEM((8, 128), F32),
            dma((2, max(N_A, N_B))),
            dma((5, N_ACC)),
            dma((5, N_ACC)),
            dma((3,)),
            dma((3,)),
            dma,
        ],
        compiler_params=pltpu.CompilerParams(collective_id=collective_id, has_side_effects=True,
                                             vmem_limit_bytes=60 * 1024 * 1024),
        name='reduce_and_direct',
    )(*grads, *stats)


N_GATH, N_W = 6, 3


def update_kernel(tiling, slots, u_in, w_qkv, w_o, w_up, w_down, n_qkv, n_o, n_up, n_down,
                  gath, w_buf, own_sem, send_sem, recv_sem, wload_sem, wstore_sem):
    me, coords, partners = place()
    core = coords[0]
    block = tiling.block
    rows = block // HALVES
    units = slots * HALVES
    weights = (w_qkv, w_o, w_up, w_down)
    results = (n_qkv, n_o, n_up, n_down)
    rest = tiling.total - (slots - 1) * RANKS

    def own(unit):
        half = unit % HALVES
        return pltpu.make_async_copy(u_in.at[unit // HALVES, pl.ds(pl.multiple_of(half * rows, rows), rows), :],
                                     gath.at[unit % N_GATH, 0], own_sem.at[unit % N_GATH])

    def remote(stage, unit):
        b = unit % N_GATH
        size = 16 >> stage
        return pltpu.make_async_remote_copy(gath.at[b, pl.ds(0, size)], gath.at[b, pl.ds(size, size)],
                                            send_sem.at[stage, b], recv_sem.at[stage, b],
                                            device_id=(partners[stage],), device_id_type=MESH)

    def each_tile(unit, fn):
        slot, half = unit // HALVES, unit % HALVES

        def one(pos, _):
            other = pos // 16
            owner = owner_at(coords, pos, core + other * (1 - 2 * core))
            number = slot * RANKS + owner

            @pl.when(number < tiling.total)
            def _():
                tiling.visit(number, half, lambda index, layer, rws, cls: fn(index, pos, layer, rws, cls))
            return 0
        lax.fori_loop(0, RANKS, one, 0)

    def w_load(unit):
        b = unit % N_W
        each_tile(unit, lambda index, pos, layer, rws, cls: pltpu.make_async_copy(
            weights[index].at[layer, rws, cls], w_buf.at[b, pos], wload_sem.at[b]).start())

    def w_store(unit):
        b = unit % N_W
        each_tile(unit, lambda index, pos, layer, rws, cls: pltpu.make_async_copy(
            w_buf.at[b, pos], results[index].at[layer, rws, cls], wstore_sem.at[b]).start())

    def w_wait(unit, sem):
        b = unit % N_W
        for count, cond in ((RANKS, unit // HALVES < slots - 1), (rest, unit // HALVES == slots - 1)):
            @pl.when(cond)
            def _():
                part = w_buf.at[b, pl.ds(0, count)]
                pltpu.make_async_copy(part, part, sem.at[b]).wait()

    def a1(unit):
        own(unit).wait()
        remote(4, unit).start()

    def step(stage, unit):
        remote(stage, unit).wait()
        remote(stage - 1, unit).start()

    def a6(unit):
        remote(0, unit).wait()
        w_wait(unit, wload_sem)

        def one(pos, _):
            w = w_buf[unit % N_W, pos]
            w_buf[unit % N_W, pos] = w - LR_RATE * (gath[unit % N_GATH, pos] + WEIGHT_DECAY * w)
            return 0
        lax.fori_loop(0, RANKS, one, 0)
        w_store(unit)

        @pl.when(unit > 0)
        def _():
            w_wait(unit - 1, wstore_sem)

        @pl.when(unit + 2 < units)
        def _():
            w_load(unit + 2)

    events = ((5, a6), (4, functools.partial(step, 1)), (3, functools.partial(step, 2)),
              (2, functools.partial(step, 3)), (1, functools.partial(step, 4)), (0, a1))

    enter(partners)
    own(0).start()
    w_load(0)
    w_load(1)

    def one_step(i, _):
        for lag, event in events:
            unit = i - lag

            @pl.when((unit >= 0) & (unit < units))
            def _(event=event, unit=unit):
                event(unit)

        @pl.when(i + 1 < units)
        def _():
            own(i + 1).start()
        return 0
    lax.fori_loop(0, units + 5, one_step, 0)
    w_wait(units - 1, wstore_sem)


def gather_and_update(tiling, direction, weights, collective_id):
    slots, block = direction.shape[0], tiling.block
    rows = block // HALVES
    hbm = pl.BlockSpec(memory_space=pl.ANY)
    dma = pltpu.SemaphoreType.DMA
    return pl.pallas_call(
        functools.partial(update_kernel, tiling, slots),
        out_shape=[jax.ShapeDtypeStruct(w.shape, F32) for w in weights],
        in_specs=[hbm] * 5,
        out_specs=[hbm] * 4,
        scratch_shapes=[
            pltpu.VMEM((N_GATH, RANKS, rows, block), F32),
            pltpu.VMEM((N_W, RANKS, rows, block), F32),
            dma((N_GATH,)),
            dma((5, N_GATH)),
            dma((5, N_GATH)),
            dma((N_W,)),
            dma((N_W,)),
        ],
        compiler_params=pltpu.CompilerParams(collective_id=collective_id, has_side_effects=True,
                                             vmem_limit_bytes=60 * 1024 * 1024),
        name='gather_and_update',
    )(direction, *weights)


def solution(mesh):
    assert mesh.shape['dp'] == RANKS

    def local_step(g_qkv, g_o, g_up, g_down, w_qkv, w_o, w_up, w_down, left_stat, right_stat, var_stat):
        weights = (w_qkv, w_o, w_up, w_down)
        slots, block = left_stat.shape[0], left_stat.shape[-1]
        tiling = Tiling([w.shape for w in weights], block)
        stats = [stat.reshape(slots, block, block) for stat in (left_stat, right_stat, var_stat)]
        left, right, var, direction = reduce_and_direct(tiling, (g_qkv, g_o, g_up, g_down), stats, 0)
        new_weights = gather_and_update(tiling, direction, weights, 1)
        return tuple(new_weights) + tuple(s.reshape(left_stat.shape) for s in (left, right, var))

    grad_spec = P('dp')
    stat_spec = P(None, 'dp')
    return jax.shard_map(local_step, mesh=mesh, in_specs=(grad_spec,) * 4 + (P(),) * 4 + (stat_spec,) * 3,
                         out_specs=(P(),) * 4 + (stat_spec,) * 3, check_vma=False)
```

time: 1900 us -> 653 us (0.34)
  waiting for transfers between devices: 908 us -> 0 us
  Pallas kernels: 0 us -> 608 us
  local copies, waits for them, and re-layouts: 526 us -> 44.5 us
  matrix products: 342 us -> 0 us
  other arithmetic: 89.8 us -> 0.01 us
    reduce_scatter x1 -> x0, waiting for transfers between devices: 617 us -> none  [local_step(): lax.psum_scatter(padded.reshape(slots, ranks, block_dim, block_dim), 'dp'...]
    pallas_call x0 -> x2, Pallas kernels: none -> 608 us  [the longest x1 347 us: reduce_and_direct(): pl.pallas_call(functools.partial(reduce_kernel, tiling, slots), out_shape...]
    dot_general x124 -> x0, matrix products: 342 us -> none  [product(): jnp.einsum(form, left_op, right_op, precision=lax.Precision.HIGHEST, pref...]
    all_gather x1 -> x0, waiting for transfers between devices: 291 us -> none  [local_step(): lax.all_gather(direction, 'dp', axis=1, tiled=True)]
    reshape x9 -> x0, local copies, waits for them, and re-layouts: 161 us -> none  [the longest x4 77.7 us: from_blocks(): tiled.transpose(0, 1, 3, 2, 4).reshape(layers, n_rows, n_cols)]
    transpose x8 -> x0, local copies, waits for them, and re-layouts: 117 us -> none  [the longest x4 72.3 us: from_blocks(): tiled.transpose(0, 1, 3, 2, 4).reshape(layers, n_rows, n_cols)]
    slice x4 -> x0, local copies, waits for them, and re-layouts: 79.3 us -> none  [the longest x3 40.7 us: from_blocks(): per_layer[:, offset:offset + tile_count]]
    sub x4 -> x0, other arithmetic: 61.4 us -> none  [local_step(): weight - LR_RATE * (step_dir + WEIGHT_DECAY * weight)]
  transfers between devices with their start and end apart: 2 -> 0, of which waited for: 2 -> 0; matrix products, arithmetic and copies ran while one was open for 2% -> 0% of each run, Pallas kernels for 0% -> 0%
where the time goes in v1:
time: 653 us
  Pallas kernels  608 us (93%)
  local copies, waits for them, and re-layouts  44.5 us (7%)
    pallas_call x1, Pallas kernels, reduce_and_direct(): pl.pallas_call(functools.partial(reduce_kernel, tiling, slots), out_shape...  347 us
    pallas_call x1, Pallas kernels, gather_and_update(): pl.pallas_call(functools.partial(update_kernel, tiling, slots), out_shape...  260 us
    unnamed x23, local copies, waits for them, and re-layouts  44.5 us

profile of v1, /device:TPU:0, one launch (start us, length us, event | category | flops | bytes accessed | tf_op | source)
XLA Modules:
  0.0 652.7 jit_solution(5152840848727286416)
XLA Ops:
  0.6 347.4 %reduce_and_direct.1 = (f32[7,256,256]{2,1,0:T(8,128)}, f32[7,256,256]{2,1,0:T(8,128)}, f32[7,256,256]{2,1,0:T(8,128)}, f32[7,256,256]{2,1,0:T(8,128)}) custom-call(bf16[2,768,2304]{2,1,0:T(8,128)(2,1)} %g_qkv.1, bf16[2,768,768]{2,1,0:T(8,128)(2,1)} %g_o.1, bf16[2,768,3072]{2,1,0:T(8,128)(2,1)} %g_up.1, bf16[2,3072,768]{2,1,0:T(8,128)(2,1)} %g_down.1, ...), custom_call_target="tpu_custom_call" | custom-call | tf_op jit(solution)/shard_map/reduce_and_direct/pallas_call | solution.py:318
  348.0 260.1 %gather_and_update.1 = (f32[2,768,2304]{2,1,0:T(8,128)}, f32[2,768,768]{2,1,0:T(8,128)}, f32[2,768,3072]{2,1,0:T(8,128)}, f32[2,3072,768]{2,1,0:T(8,128)}) custom-call(f32[7,256,256]{2,1,0:T(8,128)} %get-tuple-element.15.u_in, f32[2,768,2304]{2,1,0:T(8,128)} %w_qkv.1, f32[2,768,768]{2,1,0:T(8,128)} %w_o.1, f32[2,768,3072]{2,1,0:T(8,128)} %w_up.1, ...), custom_call_target="tpu_custom_call" | custom-call | tf_op jit(solution)/shard_map/gather_and_update/pallas_call | solution.py:466
  608.2 11.2 %copy.28 = f32[2,768,2304]{2,1,0:T(8,128)} copy(f32[2,768,2304]{2,1,0:T(8,128)} %get-tuple-element.37) | data formatting | bytes 28311552
  619.4 0.0 slice-start
  619.4 0.0 slice-start.1
  619.4 5.2 copy.29
  624.6 0.0 slice-start.2
  624.6 0.0 slice-start.3
  624.6 0.0 slice-start.4
  624.6 15.0 %copy.30 = f32[2,768,3072]{2,1,0:T(8,128)} copy(f32[2,768,3072]{2,1,0:T(8,128)} %get-tuple-element.39) | data formatting | bytes 37748736
  639.7 0.0 slice-done
  639.7 0.0 slice-done.1
  639.7 0.0 slice-done.2
  639.7 0.2 slice-done.3
  639.9 1.3 slice-done.4
  641.2 0.0 copy-start.2
  641.2 6.9 %copy.31 = f32[2,3072,768]{2,1,0:T(8,128)} copy(f32[2,3072,768]{2,1,0:T(8,128)S(1)} %bitcast.13) | data formatting | bytes 37748736
  648.0 0.0 copy-done.2
  648.1 0.0 copy-start.1
  648.1 0.0 copy-start
  648.1 1.2 copy.32
  649.3 0.9 copy-done.1
  650.2 1.2 copy.33
  651.4 0.0 copy-done
  651.4 1.2 copy.34
  (1 shorter events, 0.0 us)
Async XLA Ops:
  619.4 20.2 %slice-start = ((s8[18874368]{0:T(1024)(128)(4,1)}), s8[4194304]{0:T(1024)(128)(4,1)S(1)}, s32[]{:S(2)}) async-start(s8[18874368]{0:T(1024)(128)(4,1)} %bitcast.12), calls=%async_computation | async-start | bytes 8388608
  619.4 20.2 %slice-start.1 = ((s8[18874368]{0:T(1024)(128)(4,1)}), s8[4194304]{0:T(1024)(128)(4,1)S(1)}, s32[]{:S(2)}) async-start(s8[18874368]{0:T(1024)(128)(4,1)} %bitcast.12), calls=%async_computation.1 | async-start | bytes 8388608
  624.6 15.0 %slice-start.2 = ((s8[18874368]{0:T(1024)(128)(4,1)}), s8[4194304]{0:T(1024)(128)(4,1)S(1)}, s32[]{:S(2)}) async-start(s8[18874368]{0:T(1024)(128)(4,1)} %bitcast.12), calls=%async_computation.2 | async-start | bytes 8388608
  624.6 15.3 %slice-start.3 = ((s8[18874368]{0:T(1024)(128)(4,1)}), s8[4194304]{0:T(1024)(128)(4,1)S(1)}, s32[]{:S(2)}) async-start(s8[18874368]{0:T(1024)(128)(4,1)} %bitcast.12), calls=%async_computation.3 | async-start | bytes 8388608
  624.6 16.5 %slice-start.4 = ((s8[18874368]{0:T(1024)(128)(4,1)}), s8[2097152]{0:T(1024)(128)(4,1)S(1)}, s32[]{:S(2)}) async-start(s8[18874368]{0:T(1024)(128)(4,1)} %bitcast.12), calls=%async_computation.4 | async-start | bytes 4194304
  641.2 6.9 %copy-start.2 = (f32[7,256,256]{2,1,0:T(8,128)S(1)}, f32[7,256,256]{2,1,0:T(8,128)}, u32[]{:S(2)}) copy-start(f32[7,256,256]{2,1,0:T(8,128)} %get-tuple-element.20) | copy-start | bytes 5505028
  648.1 2.2 copy-start.1
  648.1 3.4 copy-start
